TPU v7x, 32 devices: a whole 2x2x4 slice. The times are simulated.
32 devices in a mesh: blk: 8 (over y, x, core), sub: 4 (over z).
Axes of the slice: x: 2, y: 2, z: 4, core: 2. Of those that a mesh axis runs over, the one named last changes fastest.
Arguments:
- first_core: bfloat16 [8, 128], P('blk'), may hold values from -6 to 6
- middle_core: bfloat16 [32, 32, 256], P(None, 'sub'), may hold values from -1 to 1
- last_core: bfloat16 [32, 512], replicated, may hold values from -1 to 1
- row_tt: int32 [32768], P(('blk', 'sub')), may hold values from 0 to 32767, as said below
Outputs:
- served: bfloat16 [32768, 128], P(('blk', 'sub'))
Inputs may be any that keep to these rules, and one draw needn't show every extreme that they name: `row_tt`: each window row is named exactly once. Among the rows of one device, exactly 32 entries lie in each of the 32 ranges q * 1024 to (q + 1) * 1024 - 1.
All inputs are finite; a program needn't handle non-finite values.
Results may differ from a plain program's by a relative error of at most 0.0049.
Values may be sent and summed in bfloat16 or wider, within the bound.
A program may use at most 64 MiB of HBM per device.

v0:
```python
import jax
import jax.numpy as jnp
from jax import lax
from jax.sharding import PartitionSpec as P

R = 32
J1 = 4
J2 = 8
J3 = 4


def on_device(first_core, middle_core, last_core, row_tt):
    blocks = lax.axis_size("blk")
    groups = lax.axis_size("sub")
    sources = blocks * groups
    rows_here = row_tt.shape[0]
    per_peer = rows_here // sources
    row_width = J1 * J2 * J3
    last_span = last_core.shape[1] // J3
    middle_span = middle_core.shape[1]
    first_mat = first_core.reshape(J1, R)
    partial_value = jnp.dot(
        first_mat, middle_core.reshape(R, middle_span * J2 * R), preferred_element_type=jnp.float32
    ).astype(jnp.bfloat16)
    partial_value = (
        partial_value.reshape(J1, middle_span, J2, R)
        .transpose(1, 0, 2, 3)
        .reshape(middle_span * J1 * J2, R)
    )
    products = jnp.dot(partial_value, last_core, preferred_element_type=jnp.float32).astype(
        jnp.bfloat16
    )
    products = products.reshape(middle_span, J1, J2, last_span, J3).transpose(0, 3, 1, 2, 4)
    slab_table = products.reshape(middle_span * last_span, row_width)
    owners = row_tt // rows_here
    item_index = row_tt % rows_here
    row_order = jnp.argsort(owners, stable=True)
    wanted = item_index[row_order].reshape(blocks, groups, per_peer)
    asked_rows = lax.all_to_all(
        lax.all_to_all(wanted, "blk", split_axis=0, concat_axis=0, tiled=True),
        "sub",
        split_axis=1,
        concat_axis=1,
        tiled=True,
    )
    picked = jnp.take(slab_table, asked_rows.reshape(-1), axis=0).reshape(
        blocks, groups, per_peer, row_width
    )
    arrived = lax.all_to_all(
        lax.all_to_all(picked, "blk", split_axis=0, concat_axis=0, tiled=True),
        "sub",
        split_axis=1,
        concat_axis=1,
        tiled=True,
    )
    gathered = arrived.reshape(rows_here, row_width)
    return jnp.take(gathered, jnp.argsort(row_order), axis=0)


def solution(mesh):
    placed = (P("blk", None), P(None, "sub", None), P(), P(("blk", "sub")))
    return jax.shard_map(
        on_device, mesh=mesh, in_specs=placed, out_specs=P(("blk", "sub"), None), check_vma=False
    )
```

profile of v0, /device:TPU:0, one launch (start us, length us, event | category | flops | bytes accessed | tf_op | source)
XLA Modules:
  0.0 73.1 jit_solution(8588349140319979986)
XLA Ops:
  0.0 0.0 copy-start
  0.0 0.0 copy-start.2
  0.0 0.0 copy-start.1
  0.0 0.7 %add_select_fusion = (s32[1024]{0:T(1024)S(1)}, s32[1024]{0:T(1024)S(1)}) fusion(s32[1024]{0:T(1024)} %param.9), kind=kLoop, calls=%fused_computation.11 | loop fusion | flops 19456 | bytes 12288 | tf_op jit(solution)/shard_map/jit(floor_divide)/jit(_where)/select_n | solution.py:35
  0.7 4.4 %sort.34 = (s32[1024]{0:T(1024)}, s32[1024]{0:T(1024)S(1)}) sort(s32[1024]{0:T(1024)S(1)} %get-tuple-element.10, s32[1024]{0:T(1024)S(1)} %iota.8), dimensions={0}, to_apply=%region_0.1 | sort | flops 10240 | bytes 16384 | tf_op jit(solution)/shard_map/jit(argsort)/sort | solution.py:37
  5.1 4.5 %gather_fusion = s32[1024]{0:T(1024)S(1)} fusion(s32[1024]{0:T(1024)S(1)} %get-tuple-element.11, s32[1024]{0:T(1024)S(1)} %fusion), kind=kCustom, calls=%fused_computation.2 | custom fusion | bytes 12288 | tf_op jit(solution)/shard_map/gather | solution.py:38
  9.6 0.1 reshape.41
  9.7 0.7 reshape.85
  10.4 5.2 %all-to-all-start = ((s32[8,1,128]{2,1,0:T(1,128)}), s32[8,1,128]{2,1,0:T(1,128)S(1)}, u32[]{:S(2)}, u32[]{:S(2)}) async-start(s32[8,1,128]{2,1,0:T(1,128)} %reshape.85), calls=%async_computation | async-start | bytes 8192 | tf_op jit(solution)/shard_map/all_to_all | solution.py:40
  15.6 0.6 broadcast.37
  16.2 0.0 copy-done.2
  16.2 0.7 reduce.3
  16.9 0.1 reshape.35
  17.0 0.0 copy-done.1
  17.0 0.1 convolution_convert_fusion
  17.2 0.1 reshape.37
  17.3 2.9 %all-to-all-done = s32[8,1,128]{2,1,0:T(1,128)S(1)} async-done(((s32[8,1,128]{2,1,0:T(1,128)}), s32[8,1,128]{2,1,0:T(1,128)S(1)}, u32[]{:S(2)}, u32[]{:S(2)}) %all-to-all-start) | async-done | bytes 4128 | tf_op jit(solution)/shard_map/all_to_all | solution.py:40
  20.2 0.5 broadcast.38
  20.7 0.6 reduce.4
  21.4 0.1 reshape.86
  21.5 0.7 reshape.87
  22.1 4.9 %all-to-all-start.1 = ((s32[4,1,256]{2,1,0:T(1,128)}), s32[4,1,256]{2,1,0:T(1,128)S(1)}, u32[]{:S(2)}, u32[]{:S(2)}) async-start(s32[4,1,256]{2,1,0:T(1,128)} %reshape.87), calls=%async_computation.1 | async-start | bytes 8192 | tf_op jit(solution)/shard_map/all_to_all | solution.py:39
  27.0 0.0 copy-done
  27.0 0.2 convolution_convert_fusion.1
  27.2 0.1 copy.27
  27.4 5.9 %reshape.39 = bf16[8,4,8,128,4]{2,1,0,4,3:T(4,128)(2,1)} reshape(bf16[256,512]{0,1:T(8,128)(2,1)S(1)} %copy.27) | data formatting | bytes 524288 | tf_op jit(solution)/shard_map/reshape | solution.py:33
  33.3 6.1 %copy.28 = bf16[8,128,4,8,4]{1,0,4,3,2:T(8,128)(2,1)S(1)} copy(bf16[8,128,4,8,4]{3,2,0,4,1:T(4,128)(2,1)} %bitcast.26) | data formatting | bytes 524288 | tf_op jit(solution)/shard_map/transpose | solution.py:33
  39.4 0.2 copy.29
  39.6 0.0 all-to-all-done.1
  39.6 0.6 reduce.5
  40.2 0.1 reshape.88
  40.3 0.1 reshape.42
  40.4 3.2 %gather_fusion.1 = bf16[1024,128]{1,0:T(8,128)(2,1)S(1)} fusion(bf16[1024,128]{1,0:T(8,128)(2,1)S(1)} %copy.29, s32[1024]{0:T(1024)S(1)} %fusion.2), kind=kCustom, calls=%fused_computation.clone | custom fusion | bytes 528384 | tf_op jit(solution)/shard_map/jit(_take)/gather | solution.py:46
  43.7 0.9 %broadcast_select_fusion.1 = bf16[1024,128]{1,0:T(8,128)(2,1)} fusion(bf16[1024,128]{1,0:T(8,128)(2,1)S(1)} %gather_fusion.1, pred[1024]{0:T(1024)(128)(4,1)S(1)} %compare_and_fusion.1), kind=kLoop, calls=%fused_computation.7 | loop fusion | flops 131072 | bytes 525312 | tf_op jit(solution)/shard_map/jit(_take)/select_n | solution.py:46
  44.6 3.4 %all-to-all-start.2 = ((bf16[8,4,32,128]{3,2,1,0:T(8,128)(2,1)}), bf16[8,4,32,128]{3,2,1,0:T(8,128)(2,1)S(1)}, u32[]{:S(2)}, u32[]{:S(2)}) async-start(bf16[8,4,32,128]{3,2,1,0:T(8,128)(2,1)} %bitcast.3), calls=%async_computation.2 | async-start | bytes 524288 | tf_op jit(solution)/shard_map/all_to_all | solution.py:50
  48.0 4.4 %sort.35 = (s32[1024]{0:T(1024)}, s32[1024]{0:T(1024)S(1)}) sort(s32[1024]{0:T(1024)S(1)} %get-tuple-element.8, s32[1024]{0:T(1024)S(1)} %iota.9), dimensions={0}, to_apply=%region_1.3 | sort | flops 10240 | bytes 16384 | tf_op jit(solution)/shard_map/jit(argsort)/sort | solution.py:57
  52.4 2.5 %all-to-all-done.2 = bf16[8,4,32,128]{3,2,1,0:T(8,128)(2,1)S(1)} async-done(((bf16[8,4,32,128]{3,2,1,0:T(8,128)(2,1)}), bf16[8,4,32,128]{3,2,1,0:T(8,128)(2,1)S(1)}, u32[]{:S(2)}, u32[]{:S(2)}) %all-to-all-start.2) | async-done | bytes 262176 | tf_op jit(solution)/shard_map/all_to_all | solution.py:50
  54.8 0.7 copy.30
  55.6 5.1 %all-to-all-start.3 = ((bf16[8,4,32,128]{3,2,0,1:T(8,128)(2,1)}), bf16[8,4,32,128]{3,2,0,1:T(8,128)(2,1)S(1)}, u32[]{:S(2)}, u32[]{:S(2)}) async-start(bf16[8,4,32,128]{3,2,0,1:T(8,128)(2,1)} %copy.30), calls=%async_computation.3 | async-start | bytes 524288 | tf_op jit(solution)/shard_map/all_to_all | solution.py:49
  60.7 8.3 %all-to-all-done.3 = bf16[8,4,32,128]{3,2,0,1:T(8,128)(2,1)S(1)} async-done(((bf16[8,4,32,128]{3,2,0,1:T(8,128)(2,1)}), bf16[8,4,32,128]{3,2,0,1:T(8,128)(2,1)S(1)}, u32[]{:S(2)}, u32[]{:S(2)}) %all-to-all-start.3) | async-done | bytes 262176 | tf_op jit(solution)/shard_map/all_to_all | solution.py:49
  69.0 3.2 %gather_fusion.2 = bf16[1024,128]{1,0:T(8,128)(2,1)S(1)} fusion(bf16[1024,128]{1,0:T(8,128)(2,1)S(1)} %bitcast.25, s32[1024]{0:T(1024)S(1)} %fusion.3), kind=kCustom, calls=%fused_computation.1.clone | custom fusion | bytes 528384 | tf_op jit(solution)/shard_map/jit(_take)/gather | solution.py:57
  72.2 0.9 %broadcast_select_fusion = bf16[1024,128]{1,0:T(8,128)(2,1)} fusion(bf16[1024,128]{1,0:T(8,128)(2,1)S(1)} %gather_fusion.2, pred[1024]{0:T(1024)(128)(4,1)S(1)} %compare_and_fusion), kind=kLoop, calls=%fused_computation.6 | loop fusion | flops 131072 | bytes 525312 | tf_op jit(solution)/shard_map/jit(_take)/select_n | solution.py:57
  (13 shorter events, 0.2 us)
Async XLA Ops:
  0.0 27.0 %copy-start = (bf16[32,512]{1,0:T(8,128)(2,1)S(1)}, bf16[32,512]{1,0:T(8,128)(2,1)}, u32[]{:S(2)}) copy-start(bf16[32,512]{1,0:T(8,128)(2,1)} %param.8) | copy-start | bytes 98308
  0.0 16.2 %copy-start.2 = (bf16[1,128]{1,0:T(2,128)(2,1)S(1)}, bf16[1,128]{1,0:T(2,128)(2,1)}, u32[]{:S(2)}) copy-start(bf16[1,128]{1,0:T(2,128)(2,1)} %param.6) | copy-start | bytes 772
  0.0 17.0 %copy-start.1 = (bf16[32,8,256]{2,1,0:T(8,128)(2,1)S(1)}, bf16[32,8,256]{2,1,0:T(8,128)(2,1)}, u32[]{:S(2)}) copy-start(bf16[32,8,256]{2,1,0:T(8,128)(2,1)} %param.7) | copy-start | bytes 393220
  10.4 9.8 %all-to-all-start = ((s32[8,1,128]{2,1,0:T(1,128)}), s32[8,1,128]{2,1,0:T(1,128)S(1)}, u32[]{:S(2)}, u32[]{:S(2)}) async-start(s32[8,1,128]{2,1,0:T(1,128)} %reshape.85), calls=%async_computation | async-start | bytes 8192 | tf_op jit(solution)/shard_map/all_to_all | solution.py:40
  22.1 17.5 %all-to-all-start.1 = ((s32[4,1,256]{2,1,0:T(1,128)}), s32[4,1,256]{2,1,0:T(1,128)S(1)}, u32[]{:S(2)}, u32[]{:S(2)}) async-start(s32[4,1,256]{2,1,0:T(1,128)} %reshape.87), calls=%async_computation.1 | async-start | bytes 8192 | tf_op jit(solution)/shard_map/all_to_all | solution.py:39
  44.6 10.3 %all-to-all-start.2 = ((bf16[8,4,32,128]{3,2,1,0:T(8,128)(2,1)}), bf16[8,4,32,128]{3,2,1,0:T(8,128)(2,1)S(1)}, u32[]{:S(2)}, u32[]{:S(2)}) async-start(bf16[8,4,32,128]{3,2,1,0:T(8,128)(2,1)} %bitcast.3), calls=%async_computation.2 | async-start | bytes 524288 | tf_op jit(solution)/shard_map/all_to_all | solution.py:50
  55.6 13.4 %all-to-all-start.3 = ((bf16[8,4,32,128]{3,2,0,1:T(8,128)(2,1)}), bf16[8,4,32,128]{3,2,0,1:T(8,128)(2,1)S(1)}, u32[]{:S(2)}, u32[]{:S(2)}) async-start(bf16[8,4,32,128]{3,2,0,1:T(8,128)(2,1)} %copy.30), calls=%async_computation.3 | async-start | bytes 524288 | tf_op jit(solution)/shard_map/all_to_all | solution.py:49
where the time goes:
time: 73.6 us; the launch traced here: 73.1 us
  local copies, waits for them, and re-layouts  27.1 us (37%)
  starting transfers between devices  18.6 us (25%)
  waiting for transfers between devices  13.7 us (19%)
  other arithmetic  13.3 us (18%)
    all_to_all x1, waiting for transfers between devices, on_device(): lax.all_to_all(lax.all_to_all(picked, 'blk', split_axis=0, concat_axis=0,...  8.29 us
    transpose x1, local copies, waits for them, and re-layouts, on_device(): products.reshape(middle_span, J1, J2, last_span, J3)  6.11 us
    reshape x1, local copies, waits for them, and re-layouts, on_device(): products.reshape(middle_span, J1, J2, last_span, J3)  5.89 us
    all_to_all x1, starting transfers between devices, on_device(): lax.all_to_all(wanted, 'blk', split_axis=0, concat_axis=0, tiled=True)  5.2 us
    all_to_all x1, starting transfers between devices, on_device(): lax.all_to_all(lax.all_to_all(picked, 'blk', split_axis=0, concat_axis=0,...  5.09 us
    all_to_all x1, starting transfers between devices, on_device(): lax.all_to_all(lax.all_to_all(wanted, 'blk', split_axis=0, concat_axis=0,...  4.87 us
    gather x1, local copies, waits for them, and re-layouts, on_device(): wanted = item_index[row_order].reshape(blocks, groups, per_peer)  4.52 us
    sort x1, other arithmetic, on_device(): row_order = jnp.argsort(owners, stable=True)  4.37 us
  transfers between devices with their start and end apart: 4, of which 3 were waited for; matrix products, arithmetic and copies ran while one was open for 25% of the time, Pallas kernels for 0%

commit v1 on v0

--- a/solution.py
+++ b/solution.py
@@ -1,15 +1,20 @@
+import functools
+
 import jax
 import jax.numpy as jnp
 from jax import lax
+from jax.experimental import pallas as pl
+from jax.experimental.pallas import tpu as pltpu
 from jax.sharding import PartitionSpec as P
 
 R = 32
 J1 = 4
 J2 = 8
 J3 = 4
+PARTIAL_LIMIT = 24 * 1024 * 1024
 
 
-def on_device(first_core, middle_core, last_core, row_tt):
+def exchange_rows(first_core, middle_core, last_core, row_tt):
     blocks = lax.axis_size("blk")
     groups = lax.axis_size("sub")
     sources = blocks * groups
@@ -57,6 +62,135 @@
     return jnp.take(gathered, jnp.argsort(row_order), axis=0)
 
 
+def iota(shape, axis):
+    return lax.broadcasted_iota(jnp.int32, shape, axis)
+
+
+def fill_last(last_ref, spread_ref):
+    width = J1 * J2 * J3
+    tiles = last_ref.shape[1] // width
+    per_tile = width // J3
+    stacked = jnp.concatenate(
+        [last_ref[:, t * width : (t + 1) * width] for t in range(tiles)], axis=0
+    )
+    for pair in range(per_tile // 2):
+        lane = iota((width, 2 * width), 1)
+        want = (2 * pair + lane // width) * J3 + lane % J3
+        pick = jnp.where(iota((width, 2 * width), 0) == want, 1.0, 0.0).astype(jnp.bfloat16)
+        both = jnp.dot(stacked, pick, preferred_element_type=jnp.float32)
+        for t in range(tiles):
+            for half in range(2):
+                spread_ref[t * per_tile + 2 * pair + half] = both[
+                    t * R : (t + 1) * R, half * width : (half + 1) * width
+                ]
+
+
+def fill_first(rows, wide_ref):
+    width = J1 * J2 * J3
+    lane = iota((R, width), 1)
+    own = lane % R == iota((R, width), 0)
+    spread = jnp.concatenate(
+        [jnp.where(own, jnp.broadcast_to(row, (R, width)), 0.0) for row in rows], axis=0
+    ).astype(jnp.bfloat16)
+    lane_of = iota((J1 * R, width), 1) // (J2 * J3)
+    same = jnp.where(iota((J1 * R, width), 0) // R == lane_of, 1.0, 0.0).astype(jnp.bfloat16)
+    wide = jnp.dot(spread, same, preferred_element_type=jnp.float32)
+    for i in range(len(rows)):
+        block = wide[i * R : (i + 1) * R]
+        for j in range(J2):
+            kept = jnp.where(lane // J3 % J2 == j, block, 0.0)
+            wide_ref[j * R : (j + 1) * R, i * width : (i + 1) * width] = kept.astype(jnp.bfloat16)
+
+
+def fill_partial(group, middle, wide_ref, partial_ref, middle_all):
+    width = J1 * J2 * J3
+    span = middle.shape[0] // R
+    found = jnp.dot(middle, wide_ref[...], preferred_element_type=jnp.float32)
+    found = found.astype(jnp.bfloat16).astype(jnp.float32)
+    for i in range(wide_ref.shape[1] // width):
+        for m in range(span):
+            partial_ref[i * middle_all + group * span + m] = found[
+                m * R : (m + 1) * R, i * width : (i + 1) * width
+            ]
+
+
+def serve(row_ref, partial_ref, spread_ref, sums_ref, out_ref):
+    rows_here, width = out_ref.shape
+    last_span = spread_ref.shape[0]
+    parts = R // 8
+    unroll = 16
+
+    def some_rows(step, carry):
+        for u in range(unroll):
+            k = step * unroll + u
+            row = row_ref[k]
+            left = partial_ref[row // last_span]
+            right = spread_ref[row % last_span]
+            product = left * right
+            total = product[0:8]
+            for p in range(1, parts):
+                total = total + product[8 * p : 8 * p + 8]
+            sums_ref[pl.ds(pl.multiple_of(k * 8, 8), 8), :] = total
+        return carry
+
+    lax.fori_loop(0, rows_here // unroll, some_rows, 0)
+    chunk = 128
+
+    def some_sums(step, carry):
+        base = pl.multiple_of(step * chunk * 8, chunk * 8)
+        total = sums_ref[pl.ds(base, chunk, stride=8), :]
+        for s in range(1, 8):
+            total = total + sums_ref[pl.ds(base + s, chunk, stride=8), :]
+        out_ref[pl.ds(pl.multiple_of(step * chunk, chunk), chunk), :] = total.astype(out_ref.dtype)
+        return carry
+
+    lax.fori_loop(0, rows_here // chunk, some_sums, 0)
+
+
+def build(groups, row_ref, first_ref, middle_ref, last_ref, out_ref, wide_ref, partial_ref, spread_ref, sums_ref):
+    fill_last(last_ref, spread_ref)
+    first = first_ref[...].astype(jnp.float32)
+    fill_first([first[i : i + 1] for i in range(first.shape[0])], wide_ref)
+    part = middle_ref.shape[0] // groups
+    for g in range(groups):
+        fill_partial(
+            g, middle_ref[g * part : (g + 1) * part, :], wide_ref, partial_ref, middle_ref.shape[0] // R
+        )
+    serve(row_ref, partial_ref, spread_ref, sums_ref, out_ref)
+
+
+def rebuild_rows(first_core, middle_core, last_core, row_tt):
+    blocks = lax.axis_size("blk")
+    groups = lax.axis_size("sub")
+    width = J1 * J2 * J3
+    rows_here = row_tt.shape[0]
+    span = middle_core.shape[1]
+    last_span = last_core.shape[1] // J3
+    turned = middle_core.reshape(R, span, J2, R).transpose(1, 3, 2, 0).reshape(span * R, J2 * R)
+    middle_all = lax.all_gather(turned, "sub", axis=0, tiled=True)
+    first_all = lax.all_gather(first_core, "blk", axis=0, tiled=True)
+    vmem = pl.BlockSpec(memory_space=pltpu.VMEM)
+    return pl.pallas_call(
+        functools.partial(build, groups),
+        out_shape=jax.ShapeDtypeStruct((rows_here, width), jnp.bfloat16),
+        in_specs=[pl.BlockSpec(memory_space=pltpu.SMEM), vmem, vmem, vmem],
+        out_specs=vmem,
+        scratch_shapes=[
+            pltpu.VMEM((J2 * R, blocks * width), jnp.bfloat16),
+            pltpu.VMEM((blocks * groups * span, R, width), jnp.float32),
+            pltpu.VMEM((last_span, R, width), jnp.float32),
+            pltpu.VMEM((rows_here * 8, width), jnp.float32),
+        ],
+    )(row_tt, first_all, middle_all, last_core)
+
+
+def on_device(first_core, middle_core, last_core, row_tt):
+    indices = lax.axis_size("blk") * lax.axis_size("sub") * middle_core.shape[1]
+    if indices * R * J1 * J2 * J3 * 4 > PARTIAL_LIMIT:
+        return exchange_rows(first_core, middle_core, last_core, row_tt)
+    return rebuild_rows(first_core, middle_core, last_core, row_tt)
+
+
 def solution(mesh):
     placed = (P("blk", None), P(None, "sub", None), P(), P(("blk", "sub")))
     return jax.shard_map(

time: 73.6 us -> 41.4 us (0.56)
  the two profiles are of different devices: /device:TPU:0 before, /device:TPU:1 now
where the time goes in v1:
time: 41.4 us; the launch traced here: 41 us
  blocking collectives  26.6 us (64%)
  Pallas kernels  10.8 us (26%)
  local copies, waits for them, and re-layouts  3.55 us (9%)
    all_gather x1, blocking collectives, rebuild_rows(): middle_all = lax.all_gather(turned, 'sub', axis=0, tiled=True)  15.7 us
    all_gather x1, blocking collectives, rebuild_rows(): first_all = lax.all_gather(first_core, 'blk', axis=0, tiled=True)  10.9 us
    pallas_call x1, Pallas kernels, rebuild_rows(): pl.pallas_call(functools.partial(build, groups), out_shape=jax.ShapeDtype...  10.8 us
    reshape x3, local copies, waits for them, and re-layouts, rebuild_rows(): middle_core.reshape(R, span, J2, R).transpose(1, 3, 2, 0)  2.31 us
    unnamed x3, local copies, waits for them, and re-layouts  1.24 us

profile of v1, /device:TPU:1, one launch (start us, length us, event | category | flops | bytes accessed | tf_op | source)
XLA Modules:
  0.0 41.0 jit_solution(9299522929409943091)
XLA Ops:
  0.0 1.2 %reshape.6 = bf16[32,8,8,32]{3,2,1,0:T(8,128)(2,1)S(1)} reshape(bf16[32,8,256]{2,1,0:T(8,128)(2,1)} %param.5) | data formatting | bytes 262144 | tf_op jit(solution)/shard_map/reshape | solution.py:169
  1.2 0.8 %copy.8 = bf16[32,8,8,32]{0,2,3,1:T(8,128)(2,1)S(1)} copy(bf16[32,8,8,32]{3,2,1,0:T(8,128)(2,1)S(1)} %reshape.6) | data formatting | bytes 262144 | tf_op jit(solution)/shard_map/reshape | solution.py:169
  2.0 0.4 reshape.7
  2.3 15.7 %all_gather.7.middle_ref = bf16[1024,256]{1,0:T(8,128)(2,1)} all-gather(bf16[256,256]{1,0:T(8,128)(2,1)S(1)} %reshape.7), channel_id=1, replica_groups=mesh['blk'=8,'sub'=4] {'sub'}, dimensions={0}, use_global_device_ids=true | all-gather | bytes 655360 | tf_op jit(solution)/shard_map/all_gather | solution.py:170
  18.1 0.0 copy-start
  18.1 0.7 %copy-done = bf16[1,128]{1,0:T(2,128)(2,1)S(1)} copy-done((bf16[1,128]{1,0:T(2,128)(2,1)S(1)}, bf16[1,128]{1,0:T(2,128)(2,1)}, u32[]{:S(2)}) %copy-start) | copy-done | bytes 280
  18.7 10.9 %all-gather = bf16[8,1,128]{2,1,0:T(2,128)(2,1)S(1)} all-gather(bf16[1,1,128]{2,1,0:T(2,128)(2,1)S(1)} %bitcast.9), channel_id=1, replica_groups=mesh['blk'=8,'sub'=4] {'blk'}, dimensions={0}, use_global_device_ids=true | all-gather | bytes 2304 | tf_op jit(solution)/shard_map/all_gather | solution.py:171
  29.6 0.6 %copy.11 = bf16[8,1,128]{2,0,1:T(8,128)(2,1)} copy(bf16[8,1,128]{2,1,0:T(2,128)(2,1)S(1)} %all-gather) | data formatting | bytes 4096
  30.2 10.8 %shard_map.46 = bf16[1024,128]{1,0:T(8,128)(2,1)} custom-call(s32[1024]{0:T(1024)} %row_ref.1, bf16[8,128]{1,0:T(8,128)(2,1)} %bitcast.8, bf16[1024,256]{1,0:T(8,128)(2,1)} %all_gather.7.middle_ref, bf16[32,512]{1,0:T(8,128)(2,1)} %last_ref.1), custom_call_target="tpu_custom_call" | custom-call | tf_op jit(solution)/shard_map/pallas_call | solution.py:173
Async XLA Ops:
  18.1 0.7 %copy-start = (bf16[1,128]{1,0:T(2,128)(2,1)S(1)}, bf16[1,128]{1,0:T(2,128)(2,1)}, u32[]{:S(2)}) copy-start(bf16[1,128]{1,0:T(2,128)(2,1)} %param.4) | copy-start | bytes 772

commit v2 on v1

--- a/solution.py
+++ b/solution.py
@@ -12,6 +12,7 @@
 J2 = 8
 J3 = 4
 PARTIAL_LIMIT = 24 * 1024 * 1024
+MESH = pl.DeviceIdType.MESH
 
 
 def exchange_rows(first_core, middle_core, last_core, row_tt):
@@ -117,6 +118,7 @@
 def serve(row_ref, partial_ref, spread_ref, sums_ref, out_ref):
     rows_here, width = out_ref.shape
     last_span = spread_ref.shape[0]
+    shift = last_span.bit_length() - 1
     parts = R // 8
     unroll = 16
 
@@ -124,8 +126,8 @@
         for u in range(unroll):
             k = step * unroll + u
             row = row_ref[k]
-            left = partial_ref[row // last_span]
-            right = spread_ref[row % last_span]
+            left = partial_ref[lax.shift_right_logical(row, shift)]
+            right = spread_ref[row & (last_span - 1)]
             product = left * right
             total = product[0:8]
             for p in range(1, parts):
@@ -147,16 +149,125 @@
     lax.fori_loop(0, rows_here // chunk, some_sums, 0)
 
 
-def build(groups, row_ref, first_ref, middle_ref, last_ref, out_ref, wide_ref, partial_ref, spread_ref, sums_ref):
+def turn(middle, span):
+    rows = middle.shape[0]
+    here, there = iota((rows, rows), 0), iota((rows, rows), 1)
+    same = (here // span == there % R) & (here % span == there // R)
+    order = jnp.where(same, 1.0, 0.0).astype(jnp.bfloat16)
+    flipped = lax.dot_general(
+        middle, order, (((0,), (0,)), ((), ())), preferred_element_type=jnp.float32
+    )
+    strips = []
+    for m in range(span):
+        strips.append(
+            jnp.concatenate(
+                [flipped[j * R : (j + 1) * R, m * R : (m + 1) * R] for j in range(J2)], axis=1
+            )
+        )
+    return jnp.concatenate(strips, axis=0).astype(jnp.bfloat16)
+
+
+def build(
+    blocks,
+    groups,
+    row_ref,
+    first_ref,
+    middle_ref,
+    last_ref,
+    out_ref,
+    first_all,
+    middle_all,
+    wide_ref,
+    partial_ref,
+    spread_ref,
+    sums_ref,
+    first_send,
+    first_recv,
+    far_send,
+    far_recv,
+    near_send,
+    near_recv,
+):
+    blk = lax.axis_index("blk")
+    sub = lax.axis_index("sub")
+    rows = middle_ref.shape[0]
+    span = rows // R
+    half = rows // 2
+    side = blk % 2
+    partner = blk + 1 - 2 * side
+    barrier = pltpu.get_barrier_semaphore()
+    for d in range(1, blocks):
+        pl.semaphore_signal(
+            barrier, inc=1, device_id=((blk + d) % blocks, sub), device_id_type=MESH
+        )
+    for d in range(1, groups):
+        pl.semaphore_signal(
+            barrier, inc=1, device_id=(blk, (sub + d) % groups), device_id_type=MESH
+        )
+    middle_all[sub] = turn(middle_ref[...], span)
+    first_all[blk] = first_ref[...]
+    pl.semaphore_wait(barrier, blocks + groups - 2)
+
+    def half_of(source, which):
+        return middle_all.at[source, pl.ds(pl.multiple_of(which * half, half), half)]
+
+    far = {}
+    for d in (2, 1, 3) if groups == 4 else range(1, groups):
+        far[d] = pltpu.make_async_remote_copy(
+            src_ref=half_of(sub, side),
+            dst_ref=half_of(sub, side),
+            send_sem=far_send.at[d - 1],
+            recv_sem=far_recv.at[d - 1],
+            device_id=(blk, (sub + d) % groups),
+            device_id_type=MESH,
+        )
+        far[d].start()
+    firsts = []
+    for d in range(1, blocks):
+        copy = pltpu.make_async_remote_copy(
+            src_ref=first_ref,
+            dst_ref=first_all.at[blk],
+            send_sem=first_send.at[d - 1],
+            recv_sem=first_recv.at[d - 1],
+            device_id=((blk + d) % blocks, sub),
+            device_id_type=MESH,
+        )
+        copy.start()
+        firsts.append(copy)
     fill_last(last_ref, spread_ref)
-    first = first_ref[...].astype(jnp.float32)
-    fill_first([first[i : i + 1] for i in range(first.shape[0])], wide_ref)
-    part = middle_ref.shape[0] // groups
-    for g in range(groups):
-        fill_partial(
-            g, middle_ref[g * part : (g + 1) * part, :], wide_ref, partial_ref, middle_ref.shape[0] // R
-        )
+    for copy in firsts:
+        copy.wait_recv()
+    first = [first_all[i].astype(jnp.float32) for i in range(blocks)]
+    fill_first(first, wide_ref)
+    fill_partial(sub, middle_all[sub], wide_ref, partial_ref, groups * span)
+    near = {}
+    order = [1, 3, 2] if groups == 4 else list(range(1, groups))
+    for d in order:
+        source = (sub - d + groups) % groups
+        pltpu.make_async_remote_copy(
+            src_ref=half_of(sub, side),
+            dst_ref=half_of(source, side),
+            send_sem=far_send.at[d - 1],
+            recv_sem=far_recv.at[d - 1],
+            device_id=(blk, (sub + d) % groups),
+            device_id_type=MESH,
+        ).wait_recv()
+        near[d] = pltpu.make_async_remote_copy(
+            src_ref=half_of(source, side),
+            dst_ref=half_of(source, side),
+            send_sem=near_send.at[d - 1],
+            recv_sem=near_recv.at[d - 1],
+            device_id=(partner, sub),
+            device_id_type=MESH,
+        )
+        near[d].start()
+    for d in order:
+        source = (sub - d + groups) % groups
+        near[d].wait_recv()
+        fill_partial(source, middle_all[source], wide_ref, partial_ref, groups * span)
     serve(row_ref, partial_ref, spread_ref, sums_ref, out_ref)
+    for copy in firsts + list(far.values()) + list(near.values()):
+        copy.wait_send()
 
 
 def rebuild_rows(first_core, middle_core, last_core, row_tt):
@@ -166,27 +277,36 @@
     rows_here = row_tt.shape[0]
     span = middle_core.shape[1]
     last_span = last_core.shape[1] // J3
-    turned = middle_core.reshape(R, span, J2, R).transpose(1, 3, 2, 0).reshape(span * R, J2 * R)
-    middle_all = lax.all_gather(turned, "sub", axis=0, tiled=True)
-    first_all = lax.all_gather(first_core, "blk", axis=0, tiled=True)
     vmem = pl.BlockSpec(memory_space=pltpu.VMEM)
     return pl.pallas_call(
-        functools.partial(build, groups),
+        functools.partial(build, blocks, groups),
         out_shape=jax.ShapeDtypeStruct((rows_here, width), jnp.bfloat16),
         in_specs=[pl.BlockSpec(memory_space=pltpu.SMEM), vmem, vmem, vmem],
         out_specs=vmem,
         scratch_shapes=[
+            pltpu.VMEM((blocks, 1, J1 * R), jnp.bfloat16),
+            pltpu.VMEM((groups, span * R, J2 * R), jnp.bfloat16),
             pltpu.VMEM((J2 * R, blocks * width), jnp.bfloat16),
             pltpu.VMEM((blocks * groups * span, R, width), jnp.float32),
             pltpu.VMEM((last_span, R, width), jnp.float32),
             pltpu.VMEM((rows_here * 8, width), jnp.float32),
+            pltpu.SemaphoreType.DMA((blocks - 1,)),
+            pltpu.SemaphoreType.DMA((blocks - 1,)),
+            pltpu.SemaphoreType.DMA((groups - 1,)),
+            pltpu.SemaphoreType.DMA((groups - 1,)),
+            pltpu.SemaphoreType.DMA((groups - 1,)),
+            pltpu.SemaphoreType.DMA((groups - 1,)),
         ],
-    )(row_tt, first_all, middle_all, last_core)
+        compiler_params=pltpu.CompilerParams(collective_id=0, has_side_effects=True),
+    )(row_tt, first_core, middle_core.reshape(R * span, J2 * R), last_core)
 
 
 def on_device(first_core, middle_core, last_core, row_tt):
-    indices = lax.axis_size("blk") * lax.axis_size("sub") * middle_core.shape[1]
-    if indices * R * J1 * J2 * J3 * 4 > PARTIAL_LIMIT:
+    blocks = lax.axis_size("blk")
+    indices = blocks * lax.axis_size("sub") * middle_core.shape[1]
+    last_span = last_core.shape[1] // J3
+    small = indices * R * J1 * J2 * J3 * 4 <= PARTIAL_LIMIT
+    if not small or blocks % 2 or last_span & (last_span - 1):
         return exchange_rows(first_core, middle_core, last_core, row_tt)
     return rebuild_rows(first_core, middle_core, last_core, row_tt)
 

time: 41.4 us -> 20.6 us (0.50)
  blocking collectives: 26.6 us -> 0 us
  Pallas kernels: 10.8 us -> 18.7 us
  local copies, waits for them, and re-layouts: 3.55 us -> 1.67 us
    all_gather x2 -> x0, blocking collectives: 26.6 us -> none  [the longest x1 15.7 us: rebuild_rows(): middle_all = lax.all_gather(turned, 'sub', axis=0, tiled=True)]
    pallas_call x1, Pallas kernels: 10.8 us -> 18.7 us  [rebuild_rows(): pl.pallas_call(functools.partial(build, blocks, groups), out_shape=jax.Sh...]
    reshape x3 -> x0, local copies, waits for them, and re-layouts: 2.31 us -> none  [rebuild_rows(): middle_core.reshape(R, span, J2, R).transpose(1, 3, 2, 0)]
    unnamed x3 -> x1, local copies, waits for them, and re-layouts: 1.24 us -> 1.67 us
where the time goes in v2:
time: 20.6 us; the launch traced here: 20.4 us
  Pallas kernels  18.7 us (91%)
  local copies, waits for them, and re-layouts  1.67 us (8%)
    pallas_call x1, Pallas kernels, rebuild_rows(): pl.pallas_call(functools.partial(build, blocks, groups), out_shape=jax.Sh...  18.7 us
    unnamed x1, local copies, waits for them, and re-layouts  1.67 us

profile of v2, /device:TPU:1, one launch (start us, length us, event | category | flops | bytes accessed | tf_op | source)
XLA Modules:
  0.0 20.4 jit_solution(4223364188940940441)
XLA Ops:
  0.0 18.7 %shard_map.46 = bf16[1024,128]{1,0:T(8,128)(2,1)} custom-call(s32[1024]{0:T(1024)} %row_ref.1, bf16[1,128]{1,0:T(2,128)(2,1)} %first_ref.1, bf16[256,256]{1,0:T(8,128)(2,1)} %bitcast.1, bf16[32,512]{1,0:T(8,128)(2,1)} %last_ref.1), custom_call_target="tpu_custom_call" | custom-call | tf_op jit(solution)/shard_map/pallas_call | solution.py:281
  18.7 1.7 %copy.6 = bf16[1024,128]{1,0:T(8,128)(2,1)} copy(bf16[1024,128]{1,0:T(8,128)(2,1)} %shard_map.46) | data formatting | bytes 524288

commit v3 on v2

--- a/solution.py
+++ b/solution.py
@@ -280,7 +280,7 @@
     vmem = pl.BlockSpec(memory_space=pltpu.VMEM)
     return pl.pallas_call(
         functools.partial(build, blocks, groups),
-        out_shape=jax.ShapeDtypeStruct((rows_here, width), jnp.bfloat16),
+        out_shape=pltpu.VMEM((rows_here, width), jnp.bfloat16),
         in_specs=[pl.BlockSpec(memory_space=pltpu.SMEM), vmem, vmem, vmem],
         out_specs=vmem,
         scratch_shapes=[

time: 20.6 us -> 18.9 us (0.917)
  local copies, waits for them, and re-layouts: 1.67 us -> 0.71 us
  Pallas kernels: 18.7 us -> 18.1 us
    unnamed x1, local copies, waits for them, and re-layouts: 1.67 us -> 0.71 us
    pallas_call x1, Pallas kernels: 18.7 us -> 18.1 us  [rebuild_rows(): pl.pallas_call(functools.partial(build, blocks, groups), out_shape=pltpu....]
where the time goes in v3:
time: 18.9 us; the launch traced here: 18.8 us
  Pallas kernels  18.1 us (96%)
  local copies, waits for them, and re-layouts  0.71 us (4%)
    pallas_call x1, Pallas kernels, rebuild_rows(): pl.pallas_call(functools.partial(build, blocks, groups), out_shape=pltpu....  18.1 us
    unnamed x1, local copies, waits for them, and re-layouts  0.71 us

profile of v3, /device:TPU:1, one launch (start us, length us, event | category | flops | bytes accessed | tf_op | source)
XLA Modules:
  0.0 18.8 jit_solution(17891742895549960720)
XLA Ops:
  0.0 18.1 %shard_map.46 = bf16[1024,128]{1,0:T(8,128)(2,1)S(1)} custom-call(s32[1024]{0:T(1024)} %row_ref.1, bf16[1,128]{1,0:T(2,128)(2,1)} %first_ref.1, bf16[256,256]{1,0:T(8,128)(2,1)} %bitcast.1, bf16[32,512]{1,0:T(8,128)(2,1)} %last_ref.1), custom_call_target="tpu_custom_call" | custom-call | tf_op jit(solution)/shard_map/pallas_call | solution.py:281
  18.1 0.7 %copy.6 = bf16[1024,128]{1,0:T(8,128)(2,1)} copy(bf16[1024,128]{1,0:T(8,128)(2,1)S(1)} %shard_map.46) | data formatting | bytes 524288
